TPU v7x, 32 devices: a whole 2x2x4 slice. The times are simulated.
32 devices in a mesh: region: 4 (over x, core), domain: 8 (over z, y).
Axes of the slice: x: 2, y: 2, z: 4, core: 2. Of those that a mesh axis runs over, the one named last changes fastest.
Arguments:
- midpoints: float32 [3, 16384], P(None, ('region', 'domain')), may hold values from 0 to 1, as said below
- line_vectors: float32 [3, 16384], P(None, ('region', 'domain')), may hold values from -0.09375 to 0.09375
- burgers: float32 [3, 16384], P(None, ('region', 'domain')), may hold values from -4 to 4
- destination: int32 [16384, 1], P(('region', 'domain')), may hold values from 0 to 7; in each aligned block of 512 rows (0 to 511, 512 to 1023, ...) at most 128 rows name the same one
- node_ids: int32 [2, 16384], P(None, ('region', 'domain')), may hold values from 0 to 2047
- cell_ids: int32 [16384], P(('region', 'domain')), may hold values from 0 to 127, as said below
- cell_centers: float32 [3, 512], replicated, may hold values from 0 to 1, as said below
Outputs:
- slot_traction: float32 [3, 32768], P(None, ('region', 'domain'))
- nodal_force: float32 [3, 8192], P(None, ('region', 'domain'))
Inputs may be any that keep to these rules, and one draw needn't show every extreme that they name: `destination`: among the rows of one device, no domain is named by more than 128 rows, a bound that some block reaches. `cell_ids`: region r is the slab of x from r / 4 to (r + 1) / 4 of the unit cube; its 128 cells are the boxes of a 2 x 4 x (16) grid in that slab, numbered with the last grid index fastest. `cell_centers`: each cell's center lies within its box, within a quarter of the box's width of the box's middle along each dimension. `midpoints`: each segment's midpoint lies within its cell's box.
All inputs are finite; a program needn't handle non-finite values.
Results may differ from a plain program's by a relative error of at most 0.0003.
Values sent between devices are 32-bit elements; how exact they have to be, the bound alone decides.
No kernel may reach another device: no remote copies, remote signals or barrier semaphores. Data moves between devices by JAX's collectives and lax.ppermute only.
A program may use at most 64 MiB of HBM per device.

v0:
```python
import jax
import jax.numpy as jnp
from jax import lax
from jax.sharding import PartitionSpec as P

CELLS_REG = 128
CORE2 = 0.01
EXACT = lax.Precision.HIGHEST


def product(left, right):
    return jnp.dot(left, right, precision=EXACT, preferred_element_type=jnp.float32)


def source_terms(m, l, b):
    count = m.shape[1]
    outer = (b[:, None, :] * l[None, :, :]).reshape(9, count)
    q = jnp.cross(b, l, axis=0)
    qm = (q[:, None, :] * m[None, :, :]).reshape(9, count)
    return (outer, jnp.concatenate([qm, q], axis=0))


def pair_block(m, outer, second, targets):
    r2 = (targets[0][None, :] - m[0][:, None]) ** 2
    r2 = r2 + (targets[1][None, :] - m[1][:, None]) ** 2
    r2 = r2 + (targets[2][None, :] - m[2][:, None]) ** 2
    g1 = 1.0 / jnp.sqrt(r2 + CORE2)
    g3 = g1 * g1 * g1
    first = product(outer, g1)
    other = product(second, g3)
    cross_part = (other[9:12][:, None, :] * targets[None, :, :]).reshape(9, targets.shape[1])
    return first + cross_part - other[0:9]


def moment_terms(m, l, b, centers):
    count = m.shape[1]
    outer = (b[:, None, :] * l[None, :, :]).reshape(9, count)
    offset = m - centers
    dipole = (outer[:, None, :] * offset[None, :, :]).reshape(27, count)
    q = jnp.cross(b, l, axis=0)
    return jnp.concatenate([outer, dipole, q], axis=0)


def far_field(moments, centers, region_centers, region, cells_reg):
    total = centers.shape[1]
    diffs = [region_centers[a][None, :] - centers[a][:, None] for a in range(3)]
    r2 = diffs[0] ** 2 + diffs[1] ** 2 + diffs[2] ** 2
    keep = (jnp.arange(total, dtype=jnp.int32) // cells_reg != region).astype(jnp.float32)
    g1 = keep[:, None] / jnp.sqrt(r2 + CORE2)
    g3 = g1 * g1 * g1
    field = product(moments[0:9], g1)
    pulls = []
    for axis_a in range(3):
        weighted = diffs[axis_a] * g3
        field = field + product(moments[9 + axis_a : 36 : 3], weighted)
        pulls.append(product(moments[36:39], weighted))
    nterm = jnp.stack(pulls, axis=1).reshape(9, region_centers.shape[1])
    return field + nterm


def traction(stress, b):
    count = stress.shape[1]
    sigma = stress.reshape(3, 3, count)
    sym = 0.5 * (sigma + jnp.transpose(sigma, (1, 0, 2)))
    return jnp.sum(sym * b[None, :, :], axis=1)


def fold_blocks(total_stress, rows, block_fn):
    width = rows.shape[1]
    if width <= 1024 or width % 512 != 0:
        return total_stress + block_fn(rows)
    split = jnp.transpose(rows.reshape(rows.shape[0], width // 512, 512), (1, 0, 2))

    def step(carry, part):
        return (carry + block_fn(part), None)

    result, _ = lax.scan(step, total_stress, split)
    return result


def body(midpoints, line_vectors, burgers, destination, node_ids, cell_ids, cell_centers):
    count = midpoints.shape[1]
    domains = lax.axis_size("domain")
    capacity = 2 * count // domains
    slots = 2 * count
    region = lax.axis_index("region")
    region_centers = lax.dynamic_slice_in_dim(cell_centers, region * CELLS_REG, CELLS_REG, 1)
    cell_table = (jnp.arange(CELLS_REG, dtype=jnp.int32)[:, None] == cell_ids[None, :]).astype(
        jnp.float32
    )
    seg_centers = product(region_centers, cell_table)
    feats = moment_terms(midpoints, line_vectors, burgers, seg_centers)
    partial_value = product(feats, cell_table.T)
    summed = lax.psum(partial_value, "domain")
    moments = lax.all_gather(summed, "region", axis=1, tiled=True)
    far = far_field(moments, cell_centers, region_centers, region, CELLS_REG)

    def near_stress(targets):
        empty = jnp.zeros((9, targets.shape[1]), jnp.float32)
        outer, second = source_terms(midpoints, line_vectors, burgers)
        payload = jnp.concatenate([midpoints, outer, second], axis=0)

        def expanded_block(rows):
            return pair_block(rows[0:3], rows[3:12], rows[12:24], targets)

        return fold_blocks(
            empty, lax.all_gather(payload, "domain", axis=1, tiled=True), expanded_block
        )

    dest = destination[:, 0]
    hot = (dest[:, None] == jnp.arange(domains, dtype=jnp.int32)[None, :]).astype(jnp.int32)
    rank = jnp.sum(jnp.cumsum(hot, axis=0) * hot, axis=1) - 1
    slot = dest * capacity + rank
    stress = near_stress(midpoints) + product(far, cell_table)
    force = traction(stress, burgers)
    outgoing = jnp.zeros((3, slots), jnp.float32).at[:, slot].set(force)
    slot_traction = lax.all_to_all(outgoing, "domain", split_axis=1, concat_axis=1, tiled=True)
    half = 0.5 * force
    node_partial = jnp.zeros((3, count // 2 * domains), jnp.float32)
    node_partial = node_partial.at[:, node_ids[0]].add(half).at[:, node_ids[1]].add(half)
    nodal_force = lax.psum_scatter(node_partial, "domain", scatter_dimension=1, tiled=True)
    return (slot_traction, nodal_force)


def solution(mesh):
    in_specs = (
        P(None, ("region", "domain")),
        P(None, ("region", "domain")),
        P(None, ("region", "domain")),
        P(("region", "domain"), None),
        P(None, ("region", "domain")),
        P(("region", "domain")),
        P(),
    )
    out_specs = (P(None, ("region", "domain")), P(None, ("region", "domain")))
    return jax.shard_map(body, mesh=mesh, in_specs=in_specs, out_specs=out_specs, check_vma=False)
```

profile of v0, /device:TPU:0, one launch (start us, length us, event | category | flops | bytes accessed | tf_op | source)
XLA Modules:
  0.0 186.8 jit_solution(9238915904574163798)
XLA Ops:
  9.8 38.9 %psum.7 = f32[39,128]{1,0:T(8,128)S(1)} all-reduce(f32[39,128]{1,0:T(8,128)S(1)} %fusion.27), channel_id=1, replica_groups=mesh['region'=4,'domain'=8] {'domain'}, use_global_device_ids=true, to_apply=%region_5.7 | all-reduce | flops 4992 | bytes 39936 | tf_op jit(solution)/shard_map/psum | solution.py:94
  48.7 5.3 %all_gather.7 = f32[39,512]{1,0:T(8,128)S(1)} all-gather(f32[39,128]{1,0:T(8,128)S(1)} %psum.7), channel_id=1, replica_groups=mesh['region'=4,'domain'=8] {'region'}, dimensions={1}, use_global_device_ids=true | all-gather | bytes 99840 | tf_op jit(solution)/shard_map/all_gather | solution.py:95
  56.4 31.0 %all_gather.6 = f32[24,4096]{1,0:T(8,128)S(1)} all-gather(f32[24,512]{1,0:T(8,128)S(1)} %maximum_maximum_fusion), channel_id=1, replica_groups=mesh['region'=4,'domain'=8] {'domain'}, dimensions={1}, use_global_device_ids=true | all-gather | bytes 442368 | tf_op jit(solution)/shard_map/all_gather | solution.py:107
  87.6 18.2 %while.11 = (s32[]{:T(128)}, f32[9,512]{1,0:T(8,128)S(1)}, f32[8,24,512]{2,0,1:T(8,128)S(1)}, f32[3,512]{1,0:T(4,128)S(1)}, s32[]{:T(128)}, /*index=5*/s32[]{:T(128)}, s32[]{}, s32[]{}, s32[]{}, s32[]{}) while((s32[]{:T(128)}, f32[9,512]{1,0:T(8,128)S(1)}, f32[8,24,512]{2,0,1:T(8,128)S(1)}, f32[3,512]{1,0:T(4,128)S(1)}, s32[]{:T(128)}, ...), condition=%wide.region_4.6_spmd.clone, body=%wide.region_3.5_spmd.clone.sunk | while | flops 71326208 | bytes 356539 | solution.py:77
  87.6 1.1 fusion.96
  88.8 1.0 fusion.97
  89.9 1.1 fusion.96
  92.2 1.1 fusion.96
  93.4 1.0 fusion.97
  94.5 1.1 fusion.96
  95.6 1.0 fusion.97
  96.7 1.1 fusion.96
  97.9 1.0 fusion.97
  99.0 1.1 fusion.96
  101.3 1.1 fusion.96
  103.6 1.1 fusion.96
  104.7 1.0 fusion.97
  108.4 2.5 %scatter_custom_fusion.1 = f32[3,2048]{0,1:T(8,128)S(1)} fusion(s32[512]{0:T(512)S(1)} %bitcast.138, f32[512,3]{1,0:T(8,128)S(1)} %copy.28, f32[]{:T(128)} %constant.24.clone.1), kind=kCustom, calls=%fused_computation.42 | custom fusion | flops 1536 | bytes 24580 | tf_op jit(solution)/shard_map/scatter-add | solution.py:120
  110.9 3.7 %scatter_fusion = f32[3,2048]{0,1:T(8,128)S(1)} fusion(f32[3,2048]{0,1:T(8,128)S(1)} %scatter_custom_fusion.1, s32[512]{0:T(512)S(1)} %bitcast.114, f32[512,3]{1,0:T(8,128)S(1)} %copy.28), kind=kCustom, calls=%fused_computation.2 | custom fusion | flops 1536 | bytes 20480 | tf_op jit(solution)/shard_map/scatter-add | solution.py:120
  115.6 1.1 reduce-window.6
  117.3 1.8 scatter_custom_fusion
  119.3 9.0 %all_to_all.12 = f32[3,8,128]{2,0,1:T(4,128)S(1)} all-to-all(f32[3,8,128]{2,0,1:T(4,128)S(1)} %copy.27), channel_id=1, replica_groups=mesh['region'=4,'domain'=8] {'domain'}, dimensions={1} | all-to-all | bytes 24576 | tf_op jit(solution)/shard_map/all_to_all | solution.py:117
  128.4 49.4 %reduce-scatter.2.cloned.1.call-done = f32[3,256]{0,1:T(8,128)} async-done(((f32[3,2048]{0,1:T(8,128)}), f32[3,256]{0,1:T(8,128)}) %reduce-scatter.2.cloned.1.call-update) | async-done | bytes 3088 | tf_op jit(solution)/shard_map/reduce_scatter | solution.py:121
  177.7 1.6 copy.30
  (124 shorter events, 13.9 us)
Async XLA Ops:
  7.2 0.7 copy-start.5
  7.2 170.6 %reduce-scatter.2.cloned.1.call-start = ((), (), s32[]{:S(2)}) async-start(), calls=%async_computation.2 | async-start | bytes 1179648 | tf_op jit(solution)/shard_map/reduce_scatter | solution.py:121
  7.9 0.7 copy-start.2
  7.9 0.7 copy-start.3
  8.6 0.7 copy-start.1
  8.6 0.7 copy-start.7
  107.7 0.7 copy-start.6
  114.6 1.0 copy-start
  114.6 1.0 copy-start.4
Sparse Core Ops, SparseCore 0:
  115.7 61.9 reduce-scatter.1
where the time goes:
time: 187 us
  blocking collectives  84.1 us (45%)
  waiting for transfers between devices  49.4 us (26%)
  matrix products  21.4 us (11%)
  between operations  14.3 us (8%)
  local copies, waits for them, and re-layouts  9.35 us (5%)
  other arithmetic  7.69 us (4%)
    reduce_scatter x1, waiting for transfers between devices, body(): lax.psum_scatter(node_partial, 'domain', scatter_dimension=1, tiled=True)  49.4 us
    psum x1, blocking collectives, body(): summed = lax.psum(partial_value, 'domain')  38.9 us
    all_gather x1, blocking collectives, near_stress(): lax.all_gather(payload, 'domain', axis=1, tiled=True)  31 us
    dot_general x26, matrix products, product(): jnp.dot(left, right, precision=EXACT, preferred_element_type=jnp.float32)  21.4 us
    all_to_all x1, blocking collectives, body(): lax.all_to_all(outgoing, 'domain', split_axis=1, concat_axis=1, tiled=True)  9.02 us
    scatter-add x2, other arithmetic, body(): node_partial.at[:, node_ids[0]].add(half).at[:, node_ids[1]].add(half)  6.19 us
    unnamed x19, local copies, waits for them, and re-layouts  5.89 us
    all_gather x1, blocking collectives, body(): moments = lax.all_gather(summed, 'region', axis=1, tiled=True)  5.27 us
  transfers between devices with their start and end apart: 1, of which 1 were waited for; matrix products, arithmetic and copies ran while one was open for 2% of the time, Pallas kernels for 0%

commit v1 on v0

--- a/solution.py
+++ b/solution.py
@@ -6,6 +6,15 @@
 CELLS_REG = 128
 CORE2 = 0.01
 EXACT = lax.Precision.HIGHEST
+
+
+def add_in_pairs(x, axis):
+    size = lax.axis_size(axis)
+    total, reach = (x, 1)
+    while reach < size:
+        total = total + lax.ppermute(total, axis, [(i, i ^ reach) for i in range(size)])
+        reach = 2 * reach
+    return total
 
 
 def product(left, right):
@@ -91,7 +100,7 @@
     seg_centers = product(region_centers, cell_table)
     feats = moment_terms(midpoints, line_vectors, burgers, seg_centers)
     partial_value = product(feats, cell_table.T)
-    summed = lax.psum(partial_value, "domain")
+    summed = add_in_pairs(partial_value, "domain")
     moments = lax.all_gather(summed, "region", axis=1, tiled=True)
     far = far_field(moments, cell_centers, region_centers, region, CELLS_REG)
 

time: 187 us -> 165 us (0.88)
  blocking collectives: 84.1 us -> 47.7 us
  waiting for transfers between devices: 49.4 us -> 59.8 us
  starting transfers between devices: 0.04 us -> 3.17 us
    psum x1 -> x0, blocking collectives: 38.9 us -> none  [body(): summed = lax.psum(partial_value, 'domain')]
    ppermute x0 -> x3, waiting for transfers between devices: none -> 8.42 us  [add_in_pairs(): lax.ppermute(total, axis, [(i, i ^ reach) for i in range(size)])]
    ppermute x0 -> x3, starting transfers between devices: none -> 3.13 us  [add_in_pairs(): lax.ppermute(total, axis, [(i, i ^ reach) for i in range(size)])]
    reduce_scatter x1, waiting for transfers between devices: 49.4 us -> 51.4 us  [body(): lax.psum_scatter(node_partial, 'domain', scatter_dimension=1, tiled=True)]
  transfers between devices with their start and end apart: 1 -> 4, of which waited for: 1 -> 3; matrix products, arithmetic and copies ran while one was open for 2% -> 13% of each run, Pallas kernels for 0% -> 0%
where the time goes in v1:
time: 165 us
  waiting for transfers between devices  59.8 us (36%)
  blocking collectives  47.7 us (29%)
  matrix products  21.4 us (13%)
  between operations  14.4 us (9%)
  local copies, waits for them, and re-layouts  9.49 us (6%)
  other arithmetic  8.41 us (5%)
  starting transfers between devices  3.17 us (2%)
    reduce_scatter x1, waiting for transfers between devices, body(): lax.psum_scatter(node_partial, 'domain', scatter_dimension=1, tiled=True)  51.4 us
    all_gather x1, blocking collectives, near_stress(): lax.all_gather(payload, 'domain', axis=1, tiled=True)  31.6 us
    dot_general x26, matrix products, product(): jnp.dot(left, right, precision=EXACT, preferred_element_type=jnp.float32)  21.4 us
    all_to_all x1, blocking collectives, body(): lax.all_to_all(outgoing, 'domain', split_axis=1, concat_axis=1, tiled=True)  10.9 us
    ppermute x3, waiting for transfers between devices, add_in_pairs(): lax.ppermute(total, axis, [(i, i ^ reach) for i in range(size)])  8.42 us
    scatter-add x2, other arithmetic, body(): node_partial.at[:, node_ids[0]].add(half).at[:, node_ids[1]].add(half)  6.2 us
    unnamed x19, local copies, waits for them, and re-layouts  6.05 us
    all_gather x1, blocking collectives, body(): moments = lax.all_gather(summed, 'region', axis=1, tiled=True)  5.27 us
  transfers between devices with their start and end apart: 4, of which 3 were waited for; matrix products, arithmetic and copies ran while one was open for 13% of the time, Pallas kernels for 0%

profile of v1, /device:TPU:0, one launch (start us, length us, event | category | flops | bytes accessed | tf_op | source)
XLA Modules:
  0.0 164.8 jit_solution(14092381199891915226)
XLA Ops:
  11.1 3.1 %collective-permute-start = (f32[39,128]{1,0:T(8,128)S(1)}, f32[39,128]{1,0:T(8,128)S(1)}, u32[]{:S(2)}, u32[]{:S(2)}) collective-permute-start(f32[39,128]{1,0:T(8,128)S(1)} %fusion.29), channel_id=1, source_target_pairs={{0,1},{1,0},{2,3},{3,2},{4,5},{5,4},{6,7},{7,6},{8,9},{9,8},{10,11... | collective-permute-start | bytes 59912 | tf_op jit(solution)/shard_map/ppermute | solution.py:15
  14.3 31.6 %all_gather.6 = f32[24,4096]{1,0:T(8,128)S(1)} all-gather(f32[24,512]{1,0:T(8,128)S(1)} %maximum_maximum_fusion), channel_id=1, replica_groups=mesh['region'=4,'domain'=8] {'domain'}, dimensions={1}, use_global_device_ids=true | all-gather | bytes 442368 | tf_op jit(solution)/shard_map/all_gather | solution.py:116
  46.2 18.2 %while.11 = (s32[]{:T(128)}, f32[9,512]{1,0:T(8,128)S(1)}, f32[8,24,512]{2,0,1:T(8,128)S(1)}, f32[3,512]{1,0:T(4,128)S(1)}, s32[]{:T(128)}, /*index=5*/s32[]{:T(128)}, s32[]{}, s32[]{}, s32[]{}, s32[]{}) while((s32[]{:T(128)}, f32[9,512]{1,0:T(8,128)S(1)}, f32[8,24,512]{2,0,1:T(8,128)S(1)}, f32[3,512]{1,0:T(4,128)S(1)}, s32[]{:T(128)}, ...), condition=%wide.region_4.6_spmd.clone, body=%wide.region_3.5_spmd.clone.sunk | while | flops 71326208 | bytes 356539 | solution.py:86
  46.3 1.1 fusion.100
  47.4 1.0 fusion.101
  48.5 1.1 fusion.100
  49.7 1.0 fusion.101
  50.8 1.1 fusion.100
  52.0 1.0 fusion.101
  53.1 1.1 fusion.100
  55.4 1.1 fusion.100
  57.6 1.1 fusion.100
  59.9 1.1 fusion.100
  62.2 1.1 fusion.100
  64.4 1.1 reduce-window.6
  66.0 3.8 %collective-permute-done.1 = f32[39,128]{1,0:T(8,128)S(1)} collective-permute-done((f32[39,128]{1,0:T(8,128)S(1)}, f32[39,128]{1,0:T(8,128)S(1)}, u32[]{:S(2)}, u32[]{:S(2)}) %collective-permute-start.1) | collective-permute-done | bytes 20000 | tf_op jit(solution)/shard_map/ppermute | solution.py:15
  69.8 4.7 %collective-permute-done.2 = f32[39,128]{1,0:T(8,128)S(1)} collective-permute-done((f32[39,128]{1,0:T(8,128)S(1)}, f32[39,128]{1,0:T(8,128)S(1)}, u32[]{:S(2)}, u32[]{:S(2)}) %collective-permute-start.2) | collective-permute-done | bytes 20000 | tf_op jit(solution)/shard_map/ppermute | solution.py:15
  74.5 5.3 %all_gather.7 = f32[39,512]{1,0:T(8,128)S(1)} all-gather(f32[39,128]{1,0:T(8,128)S(1)} %add.117), channel_id=1, replica_groups=mesh['region'=4,'domain'=8] {'region'}, dimensions={1}, use_global_device_ids=true | all-gather | bytes 99840 | tf_op jit(solution)/shard_map/all_gather | solution.py:104
  84.1 2.5 %scatter_custom_fusion.1 = f32[3,2048]{0,1:T(8,128)S(1)} fusion(s32[512]{0:T(512)S(1)} %bitcast.138, f32[512,3]{1,0:T(8,128)S(1)} %copy.28, f32[]{:T(128)} %constant.24.clone.1), kind=kCustom, calls=%fused_computation.42 | custom fusion | flops 1536 | bytes 24580 | tf_op jit(solution)/shard_map/scatter-add | solution.py:129
  86.7 3.7 %scatter_fusion = f32[3,2048]{0,1:T(8,128)S(1)} fusion(f32[3,2048]{0,1:T(8,128)S(1)} %scatter_custom_fusion.1, s32[512]{0:T(512)S(1)} %bitcast.114, f32[512,3]{1,0:T(8,128)S(1)} %copy.28), kind=kCustom, calls=%fused_computation.2 | custom fusion | flops 1536 | bytes 20480 | tf_op jit(solution)/shard_map/scatter-add | solution.py:129
  91.5 1.8 %scatter_custom_fusion = f32[3,1024]{0,1:T(8,128)S(1)} fusion(s32[512]{0:T(512)S(1)} %bitcast.116, f32[512,3]{1,0:T(8,128)S(1)} %copy.26, f32[]{:T(128)} %constant.24.clone.1), kind=kCustom, calls=%fused_computation.58 | custom fusion | bytes 12292 | tf_op jit(solution)/shard_map/scatter | solution.py:125
  93.6 10.9 %all_to_all.12 = f32[3,8,128]{2,0,1:T(4,128)S(1)} all-to-all(f32[3,8,128]{2,0,1:T(4,128)S(1)} %copy.27), channel_id=1, replica_groups=mesh['region'=4,'domain'=8] {'domain'}, dimensions={1} | all-to-all | bytes 24576 | tf_op jit(solution)/shard_map/all_to_all | solution.py:126
  104.4 51.4 %reduce-scatter.2.cloned.1.call-done = f32[3,256]{0,1:T(8,128)} async-done(((f32[3,2048]{0,1:T(8,128)}), f32[3,256]{0,1:T(8,128)}) %reduce-scatter.2.cloned.1.call-update) | async-done | bytes 3088 | tf_op jit(solution)/shard_map/reduce_scatter | solution.py:130
  155.8 1.6 copy.30
  (132 shorter events, 16.8 us)
Async XLA Ops:
  7.2 0.7 copy-start.2
  7.2 148.6 %reduce-scatter.2.cloned.1.call-start = ((), (), s32[]{:S(2)}) async-start(), calls=%async_computation.2 | async-start | bytes 1179648 | tf_op jit(solution)/shard_map/reduce_scatter | solution.py:130
  8.6 0.7 copy-start.5
  8.6 0.7 copy-start.1
  9.3 0.7 copy-start.7
  10.2 0.7 copy-start.3
  11.1 54.8 %collective-permute-start = (f32[39,128]{1,0:T(8,128)S(1)}, f32[39,128]{1,0:T(8,128)S(1)}, u32[]{:S(2)}, u32[]{:S(2)}) collective-permute-start(f32[39,128]{1,0:T(8,128)S(1)} %fusion.29), channel_id=1, source_target_pairs={{0,1},{1,0},{2,3},{3,2},{4,5},{5,4},{6,7},{7,6},{8,9},{9,8},{10,11... | collective-permute-start | bytes 59912 | tf_op jit(solution)/shard_map/ppermute | solution.py:15
  46.2 18.2 %copy-start.6 = (s32[2,512]{1,0:T(2,128)S(1)}, s32[2,512]{1,0:T(2,128)}, u32[]{:S(2)}) copy-start(s32[2,512]{1,0:T(2,128)} %param.15) | copy-start | bytes 12292
  46.2 18.2 %copy-start.4 = (s32[512,1]{0,1:T(1,128)S(1)}, s32[512,1]{0,1:T(1,128)}, u32[]{:S(2)}) copy-start(s32[512,1]{0,1:T(1,128)} %param.14) | copy-start | bytes 6148
  66.0 3.8 %collective-permute-start.1 = (f32[39,128]{1,0:T(8,128)S(1)}, f32[39,128]{1,0:T(8,128)S(1)}, u32[]{:S(2)}, u32[]{:S(2)}) collective-permute-start(f32[39,128]{1,0:T(8,128)S(1)} %add.115), channel_id=1, source_target_pairs={{0,2},{1,3},{2,0},{3,1},{4,6},{5,7},{6,4},{7,5},{8,10},{9,11},{10,... | collective-permute-start | bytes 59912 | tf_op jit(solution)/shard_map/ppermute | solution.py:15
  69.8 4.7 %collective-permute-start.2 = (f32[39,128]{1,0:T(8,128)S(1)}, f32[39,128]{1,0:T(8,128)S(1)}, u32[]{:S(2)}, u32[]{:S(2)}) collective-permute-start(f32[39,128]{1,0:T(8,128)S(1)} %add.116), channel_id=1, source_target_pairs={{0,4},{1,5},{2,6},{3,7},{4,0},{5,1},{6,2},{7,3},{8,12},{9,13},{10,... | collective-permute-start | bytes 59912 | tf_op jit(solution)/shard_map/ppermute | solution.py:15
  90.4 1.0 copy-start
Sparse Core Ops, SparseCore 0:
  91.5 64.2 reduce-scatter.1
